TPU v7x, 32 devices: a whole 2x2x4 slice. The times are simulated.
32 devices in a mesh: intra: 4 (over y, x), inter: 8 (over z, core).
Axes of the slice: x: 2, y: 2, z: 4, core: 2. Of those that a mesh axis runs over, the one named last changes fastest.
Arguments:
- gate_pre: bfloat16 [1536, 14336], P('intra', 'inter'), may hold values from -6 to 6
- up_pre: bfloat16 [1536, 14336], P('intra', 'inter'), may hold values from -6 to 6
- cotangent: bfloat16 [1536, 8192], P('intra'), may hold values from -6 to 6
- weight_codes: bfloat16 [8192, 14336], P('intra', 'inter'), may hold values from -0.0625 to 0.0625
- weight_scale: bfloat16 [128, 14336], P('intra', 'inter'), may hold values from 0.5 to 2
- section_one: float32 [128, 14336], P(None, 'inter'), may hold values from 1 to 20
- section_two: float32 [128, 14336], P('intra', 'inter'), may hold values from 4 to 60
Outputs:
- grad_gate: bfloat16 [1536, 14336], P('intra', 'inter')
- grad_up: bfloat16 [1536, 14336], P('intra', 'inter')
- grad_codes: float32 [8192, 14336], P(('intra', 'inter'))
All inputs are finite; a program needn't handle non-finite values.
Results may differ from a plain program's by a relative error of at most 0.015.
Values may be sent and summed in bfloat16 or wider, within the bound.
A program may use at most 256 MiB of HBM per device.

v0:
```python
import jax
import jax.numpy as jnp
from jax import lax
from jax.sharding import PartitionSpec as P

D = 8192
BLK = 64


def soft_code(values):
    return 7.0 * jnp.tanh(values / 7.0)


def dequantize(code_blocks, scales):
    matrix = code_blocks.astype(jnp.float32) * scales.astype(jnp.float32)[:, None, :]
    return matrix.astype(jnp.bfloat16).reshape(-1, code_blocks.shape[2])


def on_device(gate_pre, up_pre, cotangent, weight_codes, weight_scale, section_one, section_two):
    width_dev = weight_codes.shape[1]
    blocked = weight_codes.reshape(weight_scale.shape[0], BLK, width_dev)
    own_rows = D // lax.axis_size("intra")
    gate_rows = gate_pre.astype(jnp.float32)
    up_rows = up_pre.astype(jnp.float32)
    sigma = jax.nn.sigmoid(gate_rows)
    gated = gate_rows * sigma
    hidden = (gated * up_rows).astype(jnp.bfloat16)
    first_scale = lax.dynamic_slice_in_dim(
        section_one, lax.axis_index("intra") * (own_rows // BLK), own_rows // BLK, 0
    )
    own_layer = dequantize(blocked, weight_scale)
    columns = lax.all_to_all(cotangent, "intra", split_axis=1, concat_axis=0, tiled=True)
    partial_rows = jnp.dot(columns, own_layer, preferred_element_type=jnp.float32)
    grad_hidden = lax.psum_scatter(
        partial_rows.astype(jnp.bfloat16), "intra", scatter_dimension=0, tiled=True
    ).astype(jnp.float32)
    grad_gate = (grad_hidden * up_rows * sigma * (1.0 + gate_rows * (1.0 - sigma))).astype(
        jnp.bfloat16
    )
    grad_up = (grad_hidden * gated).astype(jnp.bfloat16)
    term = lax.dot_general(
        cotangent, hidden, (((0,), (0,)), ((), ())), preferred_element_type=jnp.float32
    )
    blocks = (
        term.reshape(own_rows * lax.axis_size("intra") // BLK, BLK, width_dev)
        / section_one[:, None, :]
    )
    group_sum = lax.psum_scatter(
        soft_code(blocks)
        .reshape(own_rows * lax.axis_size("intra"), width_dev)
        .astype(jnp.bfloat16),
        "intra",
        scatter_dimension=0,
        tiled=True,
    ).astype(jnp.float32)
    restored = group_sum.reshape(own_rows // BLK, BLK, width_dev) * first_scale[:, None, :]
    recoded = (
        soft_code(restored / section_two[:, None, :])
        .reshape(own_rows, width_dev)
        .astype(jnp.bfloat16)
    )
    owned = lax.all_to_all(recoded, "inter", split_axis=0, concat_axis=1, tiled=True)
    return (grad_gate, grad_up, owned.astype(jnp.float32))


def solution(mesh):
    placed = (
        P("intra", "inter"),
        P("intra", "inter"),
        P("intra", None),
        P("intra", "inter"),
        P("intra", "inter"),
        P(None, "inter"),
        P("intra", "inter"),
    )
    return jax.shard_map(
        on_device,
        mesh=mesh,
        in_specs=placed,
        out_specs=(P("intra", "inter"), P("intra", "inter"), P(("intra", "inter"), None)),
        check_vma=False,
    )
```

profile of v0, /device:TPU:0, one launch (start us, length us, event | category | flops | bytes accessed | tf_op | source)
XLA Modules:
  0.0 664.7 jit_solution(17766579796116984165)
XLA Ops:
  7.2 0.0 reduce-scatter.5.cloned.1.call-start
  7.2 1.8 copy.38
  9.0 1.8 copy.39
  10.9 19.7 %div.32 = f32[128,64,1792]{2,1,0:T(8,128)} broadcast(f32[128,1792]{1,0:T(8,128)} %param.12), dimensions={0,2} | broadcast | bytes 59637760 | tf_op jit(solution)/shard_map/div | solution.py:45
  30.6 57.9 %copy.40 = f32[8192,1792]{0,1:T(8,128)} copy(f32[8192,1792]{1,0:T(8,128)} %bitcast.35) | data formatting | bytes 117440512 | tf_op jit(solution)/shard_map/div | solution.py:45
  88.6 36.1 %fusion.3 = bf16[8192,1792]{0,1:T(8,128)(2,1)} fusion(f32[8192,1792]{0,1:T(8,128)} %copy.40, bf16[384,8192]{1,0:T(8,128)(2,1)} %param.9, bf16[384,1792]{0,1:T(8,128)(2,1)S(1)} %copy.38, bf16[384,1792]{0,1:T(8,128)(2,1)S(1)} %copy.39), kind=kOutput, calls=%fused_computation.4 | convolution fusion | flops 11338514432 | bytes 97124352 | tf_op jit(solution)/shard_map/dot_general | solution.py:41
  124.7 0.0 reduce-scatter.5.cloned.1.call-update
  124.7 8.7 %copy.36 = bf16[384,8192]{0,1:T(8,128)(2,1)} copy(bf16[384,8192]{1,0:T(8,128)(2,1)} %param.9) | data formatting | bytes 12582912 | tf_op args[2]
  133.3 5.5 all-to-all-start
  138.8 1.0 constant_dynamic-slice_fusion
  139.8 6.6 mul.66
  146.4 0.0 copy-start
  146.4 15.2 %copy.41 = f32[2048,1792]{0,1:T(8,128)} copy(f32[2048,1792]{1,0:T(8,128)} %bitcast.36) | data formatting | bytes 29360128 | tf_op jit(solution)/shard_map/mul | solution.py:56
  161.7 0.0 copy-done
  161.7 6.6 div.36
  168.3 0.0 copy-start.1
  168.3 15.2 %copy.42 = f32[2048,1792]{0,1:T(8,128)} copy(f32[2048,1792]{1,0:T(8,128)} %bitcast.37) | data formatting | bytes 29360128 | tf_op jit(solution)/shard_map/div | solution.py:58
  183.5 0.0 copy-done.1
  183.6 7.6 %fusion.4 = bf16[2048,1792]{1,0:T(8,128)(2,1)} fusion(bf16[2048,1792]{1,0:T(8,128)(2,1)} %param.10, f32[32,1792]{1,0:T(8,128)S(1)} %convert_element_type.54), kind=kLoop, calls=%fused_computation.6 | loop fusion | flops 11010048 | bytes 14909440 | tf_op jit(solution)/shard_map/convert_element_type | solution.py:16
  191.1 87.0 %all-to-all-done = bf16[384,4,2048]{0,2,1:T(8,128)(2,1)} async-done(((bf16[384,4,2048]{0,2,1:T(8,128)(2,1)}), bf16[384,4,2048]{0,2,1:T(8,128)(2,1)}, u32[]{:S(2)}, u32[]{:S(2)}) %all-to-all-start) | async-done | bytes 6291488 | tf_op jit(solution)/shard_map/all_to_all | solution.py:32
  278.1 8.8 %copy.37 = bf16[4,384,2048]{2,1,0:T(8,128)(2,1)} copy(bf16[4,384,2048]{1,2,0:T(8,128)(2,1)} %bitcast.2) | data formatting | bytes 12582912 | tf_op jit(solution)/shard_map/all_to_all | solution.py:32
  286.9 163.8 %reduce-scatter.5.cloned.1.call-done = bf16[2048,1792]{0,1:T(8,128)(2,1)} async-done(((bf16[8192,1792]{0,1:T(8,128)(2,1)}), bf16[2048,1792]{0,1:T(8,128)(2,1)}) %reduce-scatter.5.cloned.1.call-update) | async-done | bytes 7340048 | tf_op jit(solution)/shard_map/reduce_scatter | solution.py:48
  450.7 12.9 %multiply_convert_fusion = bf16[2048,1792]{0,1:T(8,128)(2,1)S(1)} fusion(f32[2048,1792]{0,1:T(8,128)} %copy.42, f32[2048,1792]{0,1:T(8,128)} %copy.41, bf16[2048,1792]{0,1:T(8,128)(2,1)} %reduce-scatter.5.cloned.1.call-done), kind=kLoop, calls=%fused_computation.7 | loop fusion | flops 22020096 | bytes 44040192 | tf_op jit(solution)/shard_map/convert_element_type | solution.py:60
  463.6 3.4 copy.51
  467.0 4.9 all-to-all-start.1
  471.9 0.3 reduce-scatter.7.cloned.1.call-start
  472.1 17.1 %fusion.5 = bf16[1536,1792]{0,1:T(8,128)(2,1)} fusion(bf16[2048,1792]{1,0:T(8,128)(2,1)} %fusion.4, bf16[1536,2048]{1,0:T(8,128)(2,1)} %bitcast.42), kind=kOutput, calls=%fused_computation.10 | convolution fusion | flops 11277041664 | bytes 19136512 | tf_op jit(solution)/shard_map/dot_general | solution.py:33
  489.3 8.3 %copy.47 = bf16[1536,1792]{1,0:T(8,128)(2,1)} copy(bf16[1536,1792]{0,1:T(8,128)(2,1)} %fusion.5) | data formatting | bytes 11010048
  497.5 0.0 reduce-scatter.7.cloned.1.call-update
  497.6 63.8 %reduce-scatter.7.cloned.1.call-done = bf16[384,1792]{1,0:T(8,128)(2,1)} async-done(((bf16[1536,1792]{1,0:T(8,128)(2,1)}), bf16[384,1792]{1,0:T(8,128)(2,1)}) %reduce-scatter.7.cloned.1.call-update) | async-done | bytes 1376272
  561.3 2.5 copy.48
  563.8 4.4 fusion.6
  568.2 2.5 copy.44
  570.7 2.5 copy.45
  573.2 60.1 %all-to-all-done.1 = bf16[8,256,1792]{1,2,0:T(8,128)(2,1)} async-done(((bf16[8,256,1792]{1,2,0:T(8,128)(2,1)}), bf16[8,256,1792]{1,2,0:T(8,128)(2,1)}, u32[]{:S(2)}, u32[]{:S(2)}) %all-to-all-start.1) | async-done | bytes 7340064 | tf_op jit(solution)/shard_map/all_to_all | solution.py:62
  633.3 9.6 %convert_element_type.71 = f32[8,256,1792]{1,2,0:T(8,128)} convert(bf16[8,256,1792]{1,2,0:T(8,128)(2,1)} %all-to-all-done.1) | non-fusion elementwise | flops 3670016 | bytes 22020096 | tf_op jit(solution)/shard_map/convert_element_type | solution.py:63
  642.9 15.0 %copy.46 = f32[256,14336]{1,0:T(8,128)} copy(f32[256,14336]{0,1:T(8,128)} %bitcast.38) | data formatting | bytes 29360128
  (1 shorter events, 0.0 us)
Async XLA Ops:
  7.2 443.6 %reduce-scatter.5.cloned.1.call-start = ((), (), s32[]{:S(2)}) async-start(), calls=%async_computation.4 | async-start | bytes 36700160 | tf_op jit(solution)/shard_map/reduce_scatter | solution.py:48
  133.3 144.8 %all-to-all-start = ((bf16[384,4,2048]{0,2,1:T(8,128)(2,1)}), bf16[384,4,2048]{0,2,1:T(8,128)(2,1)}, u32[]{:S(2)}, u32[]{:S(2)}) async-start(bf16[384,4,2048]{0,2,1:T(8,128)(2,1)} %bitcast.41), calls=%async_computation | async-start | bytes 12582912 | tf_op jit(solution)/shard_map/all_to_all | solution.py:32
  146.4 15.3 %copy-start = (f32[32,1792]{1,0:T(8,128)S(1)}, f32[32,1792]{1,0:T(8,128)}, u32[]{:S(2)}) copy-start(f32[32,1792]{1,0:T(8,128)} %param.13) | copy-start | bytes 688132
  168.3 15.2 %copy-start.1 = (bf16[32,1792]{1,0:T(8,128)(2,1)S(1)}, bf16[32,1792]{1,0:T(8,128)(2,1)}, u32[]{:S(2)}) copy-start(bf16[32,1792]{1,0:T(8,128)(2,1)} %param.11) | copy-start | bytes 344068
  467.0 166.3 %all-to-all-start.1 = ((bf16[8,256,1792]{1,2,0:T(8,128)(2,1)}), bf16[8,256,1792]{1,2,0:T(8,128)(2,1)}, u32[]{:S(2)}, u32[]{:S(2)}) async-start(bf16[8,256,1792]{1,2,0:T(8,128)(2,1)} %bitcast.39), calls=%async_computation.2 | async-start | bytes 14680064 | tf_op jit(solution)/shard_map/all_to_all | solution.py:62
  471.9 89.5 %reduce-scatter.7.cloned.1.call-start = ((), (), s32[]{:S(2)}) async-start(), calls=%async_computation.5 | async-start | bytes 6881280
Sparse Core Ops, SparseCore 0:
  124.8 325.8 reduce-scatter.4
  497.7 63.5 reduce-scatter.6
where the time goes:
time: 667 us; the launch traced here: 665 us
  waiting for transfers between devices  375 us (56%)
  local copies, waits for them, and re-layouts  178 us (27%)
  matrix products  53.2 us (8%)
  other arithmetic  34.4 us (5%)
  between operations  14.1 us (2%)
  starting transfers between devices  10.6 us (2%)
    reduce_scatter x1, waiting for transfers between devices, on_device(): lax.psum_scatter(soft_code(blocks).reshape(own_rows * lax.axis_size('intr...  164 us
    all_to_all x1, waiting for transfers between devices, on_device(): lax.all_to_all(cotangent, 'intra', split_axis=1, concat_axis=0, tiled=True)  87 us
    div x2, local copies, waits for them, and re-layouts, on_device(): term.reshape(own_rows * lax.axis_size('intra') // BLK, BLK, width_dev)  77.7 us
    unnamed x3, waiting for transfers between devices  63.8 us
    all_to_all x1, waiting for transfers between devices, on_device(): lax.all_to_all(recoded, 'inter', split_axis=0, concat_axis=1, tiled=True)  60.1 us
    unnamed x12, local copies, waits for them, and re-layouts  43.1 us
    dot_general x1, matrix products, on_device(): lax.dot_general(cotangent, hidden, (((0,), (0,)), ((), ())), preferred_el...  36.1 us
    mul x2, local copies, waits for them, and re-layouts, on_device(): group_sum.reshape(own_rows // BLK, BLK, width_dev) * first_scale[:, None, :]  21.9 us
  transfers between devices with their start and end apart: 4, of which 4 were waited for; matrix products, arithmetic and copies ran while one was open for 16% of the time, Pallas kernels for 0%

commit v1 on v0

v1 whole, which is shorter than its diff:
```python
import functools

import jax
import jax.numpy as jnp
from jax import lax
from jax.experimental import pallas as pl
from jax.experimental.pallas import tpu as pltpu
from jax.sharding import PartitionSpec as P


def code_rows(blk, cols_ref, hidden_ref, one_ref, two_ref, out_ref):
    groups, tok, rows = cols_ref.shape
    total = [None] * (rows // blk)
    for a in range(groups):
        term = lax.dot_general(
            cols_ref[a], hidden_ref[a * tok:(a + 1) * tok, :], (((0,), (0,)), ((), ())),
            preferred_element_type=jnp.float32,
        )
        for b in range(rows // blk):
            coded = jnp.tanh(term[b * blk:(b + 1) * blk] * (1.0 / (7.0 * one_ref[b])))
            total[b] = coded if a == 0 else total[b] + coded
    for b in range(rows // blk):
        second = 7.0 * jnp.tanh(total[b] * (one_ref[b] / two_ref[b]))
        out_ref[b * blk:(b + 1) * blk, :] = second.astype(out_ref.dtype)


def recoded_rows(cols, hidden, one, two, blk):
    groups, tok, rows = cols.shape
    width = hidden.shape[1]
    tile = min(256, rows)
    scale_spec = pl.BlockSpec((tile // blk, 1, width), lambda i: (i, 0, 0))
    return pl.pallas_call(
        functools.partial(code_rows, blk),
        grid=(rows // tile,),
        in_specs=[
            pl.BlockSpec((groups, tok, tile), lambda i: (0, 0, i)),
            pl.BlockSpec((groups * tok, width), lambda i: (0, 0)),
            scale_spec,
            scale_spec,
        ],
        out_specs=pl.BlockSpec((tile, width), lambda i: (i, 0)),
        out_shape=jax.ShapeDtypeStruct((rows, width), jnp.bfloat16),
        cost_estimate=pl.CostEstimate(
            flops=2 * rows * width * groups * tok,
            bytes_accessed=2 * (cols.size + hidden.size + rows * width),
            transcendentals=(groups + 1) * rows * width,
        ),
        compiler_params=pltpu.CompilerParams(vmem_limit_bytes=40 * 2**20),
    )(cols, hidden, one, two)


def join_rows(*refs):
    start = 0
    for ref in refs[:-1]:
        refs[-1][:, start:start + ref.shape[1]] = ref[...].astype(jnp.float32)
        start += ref.shape[1]


def joined_rows(owned):
    sources, rows, _ = owned[0].shape
    width = sum(p.shape[2] for p in owned)
    return pl.pallas_call(
        join_rows,
        grid=(sources,),
        in_specs=[pl.BlockSpec((None, rows, p.shape[2]), lambda j: (j, 0, 0)) for p in owned],
        out_specs=pl.BlockSpec((rows, width), lambda j: (0, j)),
        out_shape=jax.ShapeDtypeStruct((rows, sources * width), jnp.float32),
        cost_estimate=pl.CostEstimate(
            flops=0, bytes_accessed=6 * sources * rows * width, transcendentals=0
        ),
        compiler_params=pltpu.CompilerParams(vmem_limit_bytes=24 * 2**20),
    )(*owned)


def on_device(gate_pre, up_pre, cotangent, weight_codes, weight_scale, section_one, section_two):
    width = weight_codes.shape[1]
    n_blocks = weight_scale.shape[0]
    blk = weight_codes.shape[0] // n_blocks
    n_intra = lax.axis_size("intra")
    n_inter = lax.axis_size("inter")
    own_rows = cotangent.shape[1] // n_intra
    tok = cotangent.shape[0]
    core = lax.axis_index("inter") % 2

    half = lax.dynamic_slice_in_dim(cotangent, core * (tok // 2), tok // 2, 0)
    mine = lax.all_to_all(
        half.reshape(tok // 2, n_intra, own_rows).transpose(1, 0, 2), "intra", 0, 0
    )
    other = lax.ppermute(mine, "inter", [(i, i ^ 1) for i in range(n_inter)])
    cols = jnp.concatenate(
        [jnp.where(core == 0, mine, other), jnp.where(core == 0, other, mine)], axis=1
    )

    gate_rows = gate_pre.astype(jnp.float32)
    up_rows = up_pre.astype(jnp.float32)
    sigma = jax.nn.sigmoid(gate_rows)
    gated = gate_rows * sigma
    hidden = (gated * up_rows).astype(jnp.bfloat16)
    one = lax.dynamic_slice_in_dim(
        section_one, lax.axis_index("intra") * n_blocks, n_blocks, 0
    ).reshape(n_blocks, 1, width)
    two = section_two.reshape(n_blocks, 1, width)

    cut = width // 128 * 3 // 7 * 128
    spans = [(0, cut), (cut, width)] if cut else [(0, width)]
    gathered = []
    piece = hidden
    for lo, hi in spans:
        piece = hidden[:, lo:hi]
        if gathered:
            piece, gathered[-1] = lax.optimization_barrier((piece, gathered[-1]))
        gathered.append(lax.all_gather(piece, "intra", axis=0, tiled=True))

    pieces = []
    for (lo, hi), full in zip(spans, gathered):
        pieces.append(recoded_rows(cols, full, one[:, :, lo:hi], two[:, :, lo:hi], blk))
        if len(pieces) == 1:
            pieces[0], late_cols = lax.optimization_barrier((pieces[0], cols))

    own_layer = (
        weight_codes.reshape(n_blocks, blk, width).astype(jnp.float32)
        * weight_scale.astype(jnp.float32)[:, None, :]
    ).astype(jnp.bfloat16).reshape(-1, width)
    partial_rows = jnp.dot(
        late_cols.reshape(n_intra * tok, own_rows), own_layer, preferred_element_type=jnp.float32
    ).astype(jnp.bfloat16)
    partial_rows, _ = lax.optimization_barrier((partial_rows, gathered[-1]))
    grad_hidden = lax.psum_scatter(
        partial_rows, "intra", scatter_dimension=0, tiled=True
    ).astype(jnp.float32)
    grad_gate = (grad_hidden * up_rows * sigma * (1.0 + gate_rows * (1.0 - sigma))).astype(
        jnp.bfloat16
    )
    grad_up = (grad_hidden * gated).astype(jnp.bfloat16)

    owned = [
        lax.all_to_all(
            p.reshape(n_inter, own_rows // n_inter, p.shape[1]), "inter", 0, 0
        )
        for p in pieces
    ]
    return (grad_gate, grad_up, joined_rows(owned))


def solution(mesh):
    placed = (
        P("intra", "inter"),
        P("intra", "inter"),
        P("intra", None),
        P("intra", "inter"),
        P("intra", "inter"),
        P(None, "inter"),
        P("intra", "inter"),
    )
    return jax.shard_map(
        on_device,
        mesh=mesh,
        in_specs=placed,
        out_specs=(P("intra", "inter"), P("intra", "inter"), P(("intra", "inter"), None)),
        check_vma=False,
    )
```

time: 667 us -> 306 us (0.46)
  waiting for transfers between devices: 375 us -> 93 us
  local copies, waits for them, and re-layouts: 178 us -> 22.3 us
  blocking collectives: 0 us -> 97.8 us
  matrix products: 53.2 us -> 16.9 us
  Pallas kernels: 0 us -> 27.8 us
  other arithmetic: 34.4 us -> 23.2 us
    reduce_scatter x1, waiting for transfers between devices: 164 us -> 0.01 us  [on_device(): lax.psum_scatter(partial_rows, 'intra', scatter_dimension=0, tiled=True)]
    div x4 -> x0, local copies, waits for them, and re-layouts: 99.5 us -> none  [the longest x2 77.7 us: on_device(): term.reshape(own_rows * lax.axis_size('intra') // BLK, BLK, width_dev)]
    all_to_all x0 -> x1, blocking collectives: none -> 97.8 us  [on_device(): lax.all_to_all(p.reshape(n_inter, own_rows // n_inter, p.shape[1]), 'inte...]
    all_to_all x2, waiting for transfers between devices: 147 us -> 74.2 us  [the longest x1 39.3 us: on_device(): lax.all_to_all(half.reshape(tok // 2, n_intra, own_rows).transpose(1, 0,...]
    unnamed x3, waiting for transfers between devices: 63.8 us -> 0.05 us
    dot_general x2 -> x1, matrix products: 53.2 us -> 16.9 us  [on_device(): jnp.dot(late_cols.reshape(n_intra * tok, own_rows), own_layer, preferred_...]
    unnamed x12 -> x32, local copies, waits for them, and re-layouts: 43.1 us -> 13.7 us
    pallas_call x0 -> x3, Pallas kernels: none -> 27.8 us  [the longest x2 21.8 us: recoded_rows(): pl.pallas_call(functools.partial(code_rows, blk), grid=(rows // tile,), i...]
  transfers between devices with their start and end apart: 4 -> 6, of which waited for: 4 -> 3; matrix products, arithmetic and copies ran while one was open for 16% -> 13% of each run, Pallas kernels for 0% -> 9%
where the time goes in v1:
time: 306 us; the launch traced here: 305 us
  blocking collectives  97.8 us (32%)
  waiting for transfers between devices  93 us (30%)
  Pallas kernels  27.8 us (9%)
  other arithmetic  23.2 us (8%)
  local copies, waits for them, and re-layouts  22.3 us (7%)
  matrix products  16.9 us (6%)
  between operations  14 us (5%)
  starting transfers between devices  10.1 us (3%)
    all_to_all x1, blocking collectives, on_device(): lax.all_to_all(p.reshape(n_inter, own_rows // n_inter, p.shape[1]), 'inte...  97.8 us
    all_to_all x1, waiting for transfers between devices, on_device(): lax.all_to_all(half.reshape(tok // 2, n_intra, own_rows).transpose(1, 0,...  39.3 us
    all_to_all x1, waiting for transfers between devices, on_device(): lax.all_to_all(p.reshape(n_inter, own_rows // n_inter, p.shape[1]), 'inte...  34.9 us
    pallas_call x2, Pallas kernels, recoded_rows(): pl.pallas_call(functools.partial(code_rows, blk), grid=(rows // tile,), i...  21.8 us
    all_gather x2, waiting for transfers between devices, on_device(): gathered.append(lax.all_gather(piece, 'intra', axis=0, tiled=True))  18.8 us
    dot_general x1, matrix products, on_device(): jnp.dot(late_cols.reshape(n_intra * tok, own_rows), own_layer, preferred_...  16.9 us
    unnamed x32, local copies, waits for them, and re-layouts  13.7 us
    convert_element_type x1, other arithmetic, on_device(): own_layer = (weight_codes.reshape(n_blocks, blk, width).astype(jnp.float3...  7.61 us
  transfers between devices with their start and end apart: 6, of which 3 were waited for; matrix products, arithmetic and copies ran while one was open for 13% of the time, Pallas kernels for 9%

profile of v1, /device:TPU:0, one launch (start us, length us, event | category | flops | bytes accessed | tf_op | source)
XLA Modules:
  0.0 305.0 jit_solution(8174240332584194776)
XLA Ops:
  7.2 0.0 copy-start
  7.2 2.3 constant_dynamic-slice_fusion.1
  9.5 2.1 copy.13
  11.6 0.0 copy-start.10
  11.6 5.3 %all-to-all-start = ((bf16[4,192,2048]{2,1,0:T(8,128)(2,1)}), bf16[4,192,2048]{2,1,0:T(8,128)(2,1)}, u32[]{:S(2)}, u32[]{:S(2)}) async-start(bf16[4,192,2048]{2,1,0:T(8,128)(2,1)} %bitcast.19), calls=%async_computation | async-start | bytes 6291456 | tf_op jit(solution)/shard_map/all_to_all | solution.py:86
  16.9 0.0 all-gather.3.cloned.1.call-start
  16.9 0.0 copy-done.10
  16.9 2.2 fusion.1
  19.1 0.0 copy-start.12
  19.1 1.1 copy-done.12
  20.1 0.0 copy-start.14
  20.1 0.0 copy-start.15
  20.1 0.9 slice.25
  21.0 0.0 all-gather.3.cloned.1.call-update
  21.0 0.0 all-gather.5.cloned.1.call-start
  21.1 39.3 %all-to-all-done = bf16[4,192,2048]{2,1,0:T(8,128)(2,1)} async-done(((bf16[4,192,2048]{2,1,0:T(8,128)(2,1)}), bf16[4,192,2048]{2,1,0:T(8,128)(2,1)}, u32[]{:S(2)}, u32[]{:S(2)}) %all-to-all-start) | async-done | bytes 3145760 | tf_op jit(solution)/shard_map/all_to_all | solution.py:86
  60.4 0.0 collective-permute-start
  60.4 2.1 slice.24
  62.5 18.8 %all-gather.3.cloned.1.call-done.hidden_ref = bf16[1536,768]{1,0:T(8,128)(2,1)} async-done(((bf16[384,768]{1,0:T(8,128)(2,1)}), bf16[1536,768]{1,0:T(8,128)(2,1)}) %all-gather.3.cloned.1.call-update) | async-done | bytes 2359312 | tf_op jit(solution)/shard_map/all_gather | solution.py:112
  81.2 0.0 all-gather.5.cloned.1.call-update
  81.2 0.0 copy-done
  81.3 0.2 reshape.29
  81.5 0.0 copy-done.14
  81.5 0.2 reshape.30
  81.7 0.0 copy-start.13
  81.7 0.0 copy-done.15
  81.7 7.6 %fusion = bf16[2048,1792]{1,0:T(8,128)(2,1)} fusion(bf16[2048,1792]{1,0:T(8,128)(2,1)} %param.10, f32[32,1792]{1,0:T(8,128)S(1)} %convert_element_type.36), kind=kLoop, calls=%fused_computation.1 | loop fusion | flops 11010048 | bytes 14909440 | tf_op jit(solution)/shard_map/convert_element_type | solution.py:123
  89.4 0.0 copy-done.13
  89.4 0.0 collective-permute-done
  89.4 5.5 %broadcast_select_fusion.1 = (bf16[4,192,2048]{2,1,0:T(8,128)(2,1)S(1)}, bf16[4,192,2048]{2,1,0:T(8,128)(2,1)}) fusion(bf16[4,192,2048]{2,1,0:T(8,128)(2,1)} %all-to-all-done, bf16[4,192,2048]{2,1,0:T(8,128)(2,1)} %collective-permute-done, pred[]{:T(512)S(6)} %eq.6), kind=kLoop, calls=%fused_computation.12 | loop fusion | flops 3145728 | bytes 12582913 | tf_op jit(solution)/shard_map/jit(_where)/select_n | solution.py:91
  94.8 0.0 copy-start.9
  94.8 3.2 %pad_maximum_fusion.cols_ref = bf16[4,384,2048]{2,1,0:T(8,128)(2,1)S(1)} fusion(bf16[4,192,2048]{2,1,0:T(8,128)(2,1)} %get-tuple-element.14, bf16[4,192,2048]{2,1,0:T(8,128)(2,1)S(1)} %get-tuple-element.13), kind=kLoop, calls=%fused_computation.3 | loop fusion | flops 12582912 | bytes 12582912 | tf_op jit(solution)/shard_map/concatenate | solution.py:90
  98.0 0.0 copy-start.4
  98.0 2.6 copy-done.4
  100.6 0.0 copy-done.9
  100.6 9.7 %shard_map.94 = bf16[2048,768]{1,0:T(8,128)(2,1)S(1)} custom-call(bf16[4,384,2048]{2,1,0:T(8,128)(2,1)S(1)} %pad_maximum_fusion.cols_ref, bf16[1536,768]{1,0:T(8,128)(2,1)S(1)} %copy-done.9, f32[32,1,768]{2,1,0:T(1,128)S(1)} %slice.26.one_ref, f32[32,1,768]{2,1,0:T(1,128)S(1)} %slice.27.two_ref), custom_call_target="tpu_custom_call" | custom-call | flops 4831838208 | bytes 11796480 | tf_op jit(solution)/shard_map/pallas_call | solution.py:32
  110.4 0.0 copy-start.7
  110.4 1.6 copy-done.7
  112.0 4.7 %all-to-all-start.1 = ((bf16[8,256,768]{2,1,0:T(8,128)(2,1)}), bf16[8,256,768]{2,1,0:T(8,128)(2,1)S(1)}, u32[]{:S(2)}, u32[]{:S(2)}) async-start(bf16[8,256,768]{2,1,0:T(8,128)(2,1)} %bitcast.18), calls=%async_computation.2 | async-start | bytes 6291456 | tf_op jit(solution)/shard_map/all_to_all | solution.py:137
  116.7 0.0 reduce-scatter.2.cloned.1.call-start
  116.7 16.9 %convolution_convert_fusion = bf16[1536,1792]{1,0:T(8,128)(2,1)} fusion(bf16[1536,2048]{1,0:T(8,128)(2,1)} %bitcast.16, bf16[2048,1792]{1,0:T(8,128)(2,1)} %fusion), kind=kOutput, calls=%fused_computation.2 | convolution fusion | flops 11277041664 | bytes 19136512 | tf_op jit(solution)/shard_map/dot_general | solution.py:124
  133.6 0.0 all-gather.5.cloned.1.call-done.hidden_ref
  133.6 0.0 reduce-scatter.2.cloned.1.call-update
  133.6 0.9 slice.29.two_ref
  134.5 0.0 copy-start.5
  134.6 2.8 copy-done.5
  137.3 0.0 copy-start.8
  137.3 1.9 copy-done.8
  139.2 12.0 %shard_map.95 = bf16[2048,1024]{1,0:T(8,128)(2,1)S(1)} custom-call(bf16[4,384,2048]{2,1,0:T(8,128)(2,1)S(1)} %copy-done.5, bf16[1536,1024]{1,0:T(8,128)(2,1)S(1)} %copy-done.8, f32[32,1,1024]{2,1,0:T(1,128)S(1)} %slice.28.one_ref, f32[32,1,1024]{2,1,0:T(1,128)S(1)} %slice.29.two_ref), custom_call_target="tpu_custom_call" | custom-call | flops 6442450944 | bytes 13631488 | tf_op jit(solution)/shard_map/pallas_call | solution.py:32
  151.3 0.0 copy-start.6
  151.3 2.0 copy-done.6
  153.3 34.9 %all-to-all-done.1.refs_0_ = bf16[8,256,768]{2,1,0:T(8,128)(2,1)S(1)} async-done(((bf16[8,256,768]{2,1,0:T(8,128)(2,1)}), bf16[8,256,768]{2,1,0:T(8,128)(2,1)S(1)}, u32[]{:S(2)}, u32[]{:S(2)}) %all-to-all-start.1) | async-done | bytes 3145760 | tf_op jit(solution)/shard_map/all_to_all | solution.py:137
  188.2 0.0 copy-start.2
  188.2 1.6 copy-done.2
  189.8 0.0 copy-start.3
  189.8 97.8 %all_to_all.15.refs_1_ = bf16[8,256,1024]{2,1,0:T(8,128)(2,1)S(1)} all-to-all(bf16[8,256,1024]{2,1,0:T(8,128)(2,1)} %bitcast.17), channel_id=1, replica_groups=mesh['intra'=4,'inter'=8] {'inter'}, dimensions={0} | all-to-all | bytes 8388608 | tf_op jit(solution)/shard_map/all_to_all | solution.py:137
  287.7 0.0 copy-done.3
  287.7 0.0 copy-start.11
  287.7 0.0 copy-start.1
  287.7 6.1 %shard_map.96 = f32[256,14336]{1,0:T(8,128)} custom-call(bf16[8,256,768]{2,1,0:T(8,128)(2,1)S(1)} %copy-done.3, bf16[8,256,1024]{2,1,0:T(8,128)(2,1)S(1)} %all_to_all.15.refs_1_), custom_call_target="tpu_custom_call" | custom-call | bytes 22020096 | tf_op jit(solution)/shard_map/pallas_call | solution.py:62
  293.7 0.0 reduce-scatter.2.cloned.1.call-done
  293.7 0.0 copy-done.11
  293.7 4.7 %fusion.5 = (bf16[384,1792]{1,0:T(8,128)(2,1)}, bf16[384,1792]{1,0:T(8,128)(2,1)}) fusion(bf16[384,1792]{1,0:T(8,128)(2,1)} %reduce-scatter.2.cloned.1.call-done, bf16[384,1792]{1,0:T(8,128)(2,1)} %param.7, bf16[384,1792]{1,0:T(8,128)(2,1)S(1)} %copy-done.11), kind=kLoop, calls=%fused_computation.17 | loop fusion | flops 11010048 | bytes 6881280 | tf_op jit(solution)/shard_map/convert_element_type | solution.py:134
  298.5 0.0 copy-done.1
  (5 shorter events, 0.1 us)
Async XLA Ops:
  7.2 74.1 %copy-start = (f32[128,1792]{1,0:T(8,128)S(1)}, f32[128,1792]{1,0:T(8,128)}, u32[]{:S(2)}) copy-start(f32[128,1792]{1,0:T(8,128)} %param.12) | copy-start | bytes 2752516
  11.6 5.3 %copy-start.10 = (bf16[384,1792]{1,0:T(8,128)(2,1)S(1)}, bf16[384,1792]{1,0:T(8,128)(2,1)}, u32[]{:S(2)}) copy-start(bf16[384,1792]{1,0:T(8,128)(2,1)} %param.8) | copy-start | bytes 4128772
  11.6 48.8 %all-to-all-start = ((bf16[4,192,2048]{2,1,0:T(8,128)(2,1)}), bf16[4,192,2048]{2,1,0:T(8,128)(2,1)}, u32[]{:S(2)}, u32[]{:S(2)}) async-start(bf16[4,192,2048]{2,1,0:T(8,128)(2,1)} %bitcast.19), calls=%async_computation | async-start | bytes 6291456 | tf_op jit(solution)/shard_map/all_to_all | solution.py:86
  16.9 64.3 %all-gather.3.cloned.1.call-start = ((), (), s32[]{:S(2)}) async-start(), calls=%async_computation.4 | async-start | bytes 2949120 | tf_op jit(solution)/shard_map/all_gather | solution.py:112
  19.1 1.1 copy-start.12
  20.1 61.3 %copy-start.14 = (f32[32,1792]{1,0:T(8,128)S(1)}, f32[32,1792]{1,0:T(8,128)}, u32[]{:S(2)}) copy-start(f32[32,1792]{1,0:T(8,128)} %param.13) | copy-start | bytes 688132
  20.1 61.6 %copy-start.15 = (bf16[32,1792]{1,0:T(8,128)(2,1)S(1)}, bf16[32,1792]{1,0:T(8,128)(2,1)}, u32[]{:S(2)}) copy-start(bf16[32,1792]{1,0:T(8,128)(2,1)} %param.11) | copy-start | bytes 344068
  21.0 112.5 %all-gather.5.cloned.1.call-start = ((), (), s32[]{:S(2)}) async-start(), calls=%async_computation.5 | async-start | bytes 3932160 | tf_op jit(solution)/shard_map/all_gather | solution.py:112
  60.4 29.0 %collective-permute-start = (bf16[4,192,2048]{2,1,0:T(8,128)(2,1)}, bf16[4,192,2048]{2,1,0:T(8,128)(2,1)}, u32[]{:S(2)}, u32[]{:S(2)}) collective-permute-start(bf16[4,192,2048]{2,1,0:T(8,128)(2,1)} %all-to-all-done), channel_id=1, source_target_pairs={{0,1},{1,0},{2,3},{3,2},{4,5},{5,4},{6,7},{7,6},{8,9},{9,8},{10,11... | collective-permute-start | bytes 9437192 | tf_op jit(solution)/shard_map/ppermute | solution.py:89
  81.7 7.7 %copy-start.13 = (f32[32,1,1792]{2,1,0:T(1,128)}, f32[32,1,1792]{2,1,0:T(1,128)S(1)}, u32[]{:S(2)}) copy-start(f32[32,1,1792]{2,1,0:T(1,128)S(1)} %reshape.30) | copy-start | bytes 688132
  94.8 5.8 %copy-start.9 = (bf16[1536,768]{1,0:T(8,128)(2,1)S(1)}, bf16[1536,768]{1,0:T(8,128)(2,1)}, u32[]{:S(2)}) copy-start(bf16[1536,768]{1,0:T(8,128)(2,1)} %all-gather.3.cloned.1.call-done.hidden_ref) | copy-start | bytes 7077892
  98.0 2.6 copy-start.4
  110.4 1.6 copy-start.7
  112.0 76.2 %all-to-all-start.1 = ((bf16[8,256,768]{2,1,0:T(8,128)(2,1)}), bf16[8,256,768]{2,1,0:T(8,128)(2,1)S(1)}, u32[]{:S(2)}, u32[]{:S(2)}) async-start(bf16[8,256,768]{2,1,0:T(8,128)(2,1)} %bitcast.18), calls=%async_computation.2 | async-start | bytes 6291456 | tf_op jit(solution)/shard_map/all_to_all | solution.py:137
  116.7 177.0 %reduce-scatter.2.cloned.1.call-start = ((), (), s32[]{:S(2)}) async-start(), calls=%async_computation.6 | async-start | bytes 6881280 | tf_op jit(solution)/shard_map/reduce_scatter | solution.py:128
  134.5 2.8 copy-start.5
  137.3 1.9 copy-start.8
  151.3 2.0 copy-start.6
  188.2 1.6 copy-start.2
  189.8 97.8 %copy-start.3 = (bf16[8,256,768]{2,1,0:T(8,128)(2,1)S(1)}, bf16[8,256,768]{2,1,0:T(8,128)(2,1)}, u32[]{:S(2)}) copy-start(bf16[8,256,768]{2,1,0:T(8,128)(2,1)} %copy-done.2) | copy-start | bytes 9437188
  287.7 6.1 %copy-start.11 = (bf16[384,1792]{1,0:T(8,128)(2,1)S(1)}, bf16[384,1792]{1,0:T(8,128)(2,1)}, u32[]{:S(2)}) copy-start(bf16[384,1792]{1,0:T(8,128)(2,1)} %param.8) | copy-start | bytes 4128772
  287.7 10.8 %copy-start.1 = (f32[128,1792]{1,0:T(8,128)S(1)}, f32[128,1792]{1,0:T(8,128)}, u32[]{:S(2)}) copy-start(f32[128,1792]{1,0:T(8,128)} %param.12) | copy-start | bytes 2752516
Sparse Core Ops, SparseCore 0:
  21.2 59.9 all-gather.2
  83.6 43.8 all-gather.4
  133.7 63.9 reduce-scatter.1
